TPU v7x, 32 devices: a whole 2x2x4 slice. The times are simulated.
32 devices in a mesh: freq: 16 (over z, x, core), grid: 2 (over y).
Axes of the slice: x: 2, y: 2, z: 4, core: 2. Of those that a mesh axis runs over, the one named last changes fastest.
Arguments:
- cross_spectra: float32 [2, 32, 256, 256], P(None, None, 'freq', 'grid'), as said below
- sensor_modes: float32 [32, 96, 256], P('freq', None, 'grid'), may hold values from -0.375 to 0.375
- source_modes: float32 [32, 96, 256], P('freq', None, 'grid'), may hold values from -6 to 6
- wavenumber: float32 [32, 96], P('freq'), may hold values from 0.5 to 2
- attenuation: float32 [32, 96], P('freq'), may hold values from 0.002 to 0.03
- mode_counts: int32 [32], P('freq'), may hold values from 48 to 96
Outputs:
- bartlett_power: float32 [64, 256], P('freq', 'grid')
Inputs may be any that keep to these rules, and one draw needn't show every extreme that they name: `cross_spectra`: each bin's matrix K_f is Hermitian and positive definite. Modes with index mode_counts[f] or more are left out in bin f.
All inputs are finite; a program needn't handle non-finite values.
Results may differ from a plain program's by a relative error of at most 0.0003.
Values sent between devices are 32-bit elements; how exact they have to be, the bound alone decides.
A program may use at most 128 MiB of HBM per device.

v0:
```python
import jax
import jax.numpy as jnp
from jax import lax
from jax.sharding import PartitionSpec as P

RANGES = 64
HIGH = lax.Precision.HIGHEST


def replica_terms(wave_row, atten_row, count, source_row, ranges):
    phase = wave_row[:, None] * ranges[None, :]
    magnitude = jnp.exp(-atten_row[:, None] * ranges[None, :]) / jnp.sqrt(phase)
    keep = (jnp.arange(source_row.shape[0], dtype=jnp.int32) < count).astype(jnp.float32)
    hankel_real = magnitude * jnp.cos(phase) * keep[:, None]
    hankel_imag = magnitude * jnp.sin(phase) * keep[:, None]
    coef_real = hankel_real[:, :, None] * source_row[:, None, :]
    coef_imag = hankel_imag[:, :, None] * source_row[:, None, :]
    return (coef_real, coef_imag)


def per_device(cross_spectra, sensor_modes, source_modes, wavenumber, attenuation, mode_counts):
    modes = sensor_modes.shape[1]
    bins_here = sensor_modes.shape[0]
    depth_here = source_modes.shape[2]
    total_bins = bins_here * lax.axis_size("freq")
    whole_spectra = lax.all_to_all(
        lax.all_to_all(cross_spectra, "freq", split_axis=1, concat_axis=2, tiled=True),
        "grid",
        split_axis=1,
        concat_axis=3,
        tiled=True,
    )
    whole_modes = lax.all_to_all(sensor_modes, "grid", split_axis=0, concat_axis=2, tiled=True)
    product = jnp.einsum("cbij,bmj->cbim", whole_spectra, whole_modes, precision=HIGH)
    projected = jnp.einsum("bmi,cbin->cbmn", whole_modes, product, precision=HIGH)
    gram = jnp.einsum("bmi,bni->bmn", whole_modes, whole_modes, precision=HIGH)
    stacked_local = jnp.concatenate([projected, gram[None]], 0)
    spectra = lax.all_gather(stacked_local, "grid", axis=1, tiled=True)
    count = RANGES // lax.axis_size("freq") * lax.axis_size("freq")
    ranges = 1.0 + jnp.arange(count, dtype=jnp.int32).astype(jnp.float32)

    def one_bin(bin_index, total):
        block = spectra[:, bin_index]
        coupling = jnp.concatenate(
            [jnp.concatenate([block[0], -block[1]], 1), jnp.concatenate([block[1], block[0]], 1)], 0
        )
        coef_real, coef_imag = replica_terms(
            wavenumber[bin_index],
            attenuation[bin_index],
            mode_counts[bin_index],
            source_modes[bin_index],
            ranges,
        )
        coefs = jnp.concatenate([coef_real, coef_imag], 0).reshape(2 * modes, count * depth_here)
        image = jnp.dot(coupling, coefs, precision=HIGH)
        weighted = jnp.einsum(
            "mn,cnx->cmx", block[2], coefs.reshape(2, modes, count * depth_here), precision=HIGH
        )
        weighted = weighted.reshape(2 * modes, count * depth_here)
        numer = jnp.sum(coefs * image, axis=0)
        denom = jnp.sum(coefs * weighted, axis=0)
        return total + (numer / denom).reshape(count, depth_here)

    summed = lax.fori_loop(0, bins_here, one_bin, jnp.zeros((count, depth_here), jnp.float32))
    return lax.psum_scatter(summed / total_bins, "freq", scatter_dimension=0, tiled=True)


def solution(mesh):
    placed = (
        P(None, None, "freq", "grid"),
        P("freq", None, "grid"),
        P("freq", None, "grid"),
        P("freq", None),
        P("freq", None),
        P("freq"),
    )
    return jax.shard_map(
        per_device, mesh=mesh, in_specs=placed, out_specs=P("freq", "grid"), check_vma=False
    )
```

profile of v0, /device:TPU:0, one launch (start us, length us, event | category | flops | bytes accessed | tf_op | source)
XLA Modules:
  0.0 178.7 jit_solution(12962401052543887064)
XLA Ops:
  0.0 0.0 copy-start.2
  0.0 0.0 copy-start.3
  0.0 0.0 copy-start.4
  0.0 0.0 copy-start.1
  0.0 1.1 copy.23
  1.2 21.5 %all_to_all.48 = f32[2,32,16,128]{3,2,0,1:T(8,128)S(1)} all-to-all(f32[2,32,16,128]{3,2,0,1:T(8,128)S(1)} %copy.23), channel_id=1, replica_groups=mesh['freq'=16,'grid'=2] {'freq'}, dimensions={1} | all-to-all | bytes 1048576 | tf_op jit(solution)/shard_map/all_to_all | solution.py:27
  22.6 3.3 %all-to-all-start = ((f32[2,96,128]{2,1,0:T(8,128)}), f32[2,96,128]{2,1,0:T(8,128)S(1)}, u32[]{:S(2)}, u32[]{:S(2)}) async-start(f32[2,96,128]{2,1,0:T(8,128)} %param.9), calls=%async_computation | async-start | bytes 196608 | tf_op jit(solution)/shard_map/all_to_all | solution.py:33
  26.0 0.8 copy.24
  26.8 3.4 %all-to-all-done = f32[2,96,128]{2,1,0:T(8,128)S(1)} async-done(((f32[2,96,128]{2,1,0:T(8,128)}), f32[2,96,128]{2,1,0:T(8,128)S(1)}, u32[]{:S(2)}, u32[]{:S(2)}) %all-to-all-start) | async-done | bytes 98336 | tf_op jit(solution)/shard_map/all_to_all | solution.py:33
  30.3 3.5 %all-to-all-start.2 = ((f32[2,2,256,128]{3,2,0,1:T(8,128)}), f32[2,2,256,128]{3,2,0,1:T(8,128)S(1)}, u32[]{:S(2)}, u32[]{:S(2)}) async-start(f32[2,2,256,128]{3,2,0,1:T(8,128)} %bitcast.6), calls=%async_computation.2 | async-start | bytes 1048576 | tf_op jit(solution)/shard_map/all_to_all | solution.py:26
  33.8 1.3 dynamic-slice
  35.8 0.1 copy.26
  35.8 0.1 reshape.252
  35.9 0.2 convolution_bitcast_fusion.3
  36.2 5.0 %all-to-all-done.2 = f32[2,2,256,128]{3,2,0,1:T(8,128)S(1)} async-done(((f32[2,2,256,128]{3,2,0,1:T(8,128)}), f32[2,2,256,128]{3,2,0,1:T(8,128)S(1)}, u32[]{:S(2)}, u32[]{:S(2)}) %all-to-all-start.2) | async-done | bytes 524320 | tf_op jit(solution)/shard_map/all_to_all | solution.py:26
  41.1 0.6 convolution_bitcast_fusion.1
  41.8 0.3 convolution_bitcast_fusion.2
  42.1 0.1 copy.28
  42.2 5.8 %all_gather.3 = f32[3,2,96,96]{3,2,0,1:T(8,128)S(1)} all-gather(f32[3,1,96,96]{3,2,0,1:T(8,128)S(1)} %copy.28), channel_id=1, replica_groups=mesh['freq'=16,'grid'=2] {'grid'}, dimensions={1}, use_global_device_ids=true | all-gather | bytes 331776 | tf_op jit(solution)/shard_map/all_gather | solution.py:38
  48.0 0.0 copy-done.2
  48.0 0.0 copy-done.3
  48.0 0.0 copy-done.4
  48.1 0.0 copy-done.1
  48.1 72.4 %while.15 = (s32[]{:T(128)}, f32[64,128]{1,0:T(8,128)S(1)}, f32[2,96]{1,0:T(2,128)S(1)}, f32[2,96]{1,0:T(2,128)S(1)}, s32[2]{0:T(128)S(1)}, /*index=5*/f32[2,96,...) while((s32[]{:T(128)}, f32[64,128]{1,0:T(8,128)S(1)}, ...), condition=%wide.region_3.0_spmd.clone.clone, body=%wide.region_0.0_spmd.clone.clone.sunk | while | flops 5445426688 | bytes 89226920 | solution.py:64
  48.1 0.6 dynamic_slice.62
  48.7 0.6 compare_convert_fusion.2
  49.3 0.2 fusion.42
  49.5 0.1 copy.48
  49.6 0.1 copy.49
  49.7 1.8 %broadcast_multiply_fusion.4 = (f32[96,64,128]{2,1,0:T(8,128)S(1)}, f32[96,64,128]{2,1,0:T(8,128)S(1)}) fusion(f32[96,64]{1,0:T(8,128)S(1)} %copy.48, f32[96,128]{1,0:T(8,128)S(1)} %dynamic-slice_bitcast_fusion.4, f32[96,64]{1,0:T(8,128)S(1)} %copy.49), kind=kLoop, calls=%fused_computation.9.clone.1 | loop fusion | flops 1572864 | bytes 6389760 | tf_op jit(solution)/shard_map/while/body/eval_jaxpr/mul | solution.py:17
  51.5 2.2 %bitcast_dynamic-update-slice_fusion.4 = f32[192,8192]{1,0:T(8,128)S(1)} fusion(f32[12,8,64,128]{3,2,1,0:T(8,128)S(1)} %bitcast.112), kind=kLoop, calls=%fused_computation.6.clone.1 | loop fusion | bytes 6291456 | tf_op jit(solution)/shard_map/while
  53.7 2.2 %bitcast_dynamic-update-slice_fusion.5 = f32[192,8192]{1,0:T(8,128)S(1)} fusion(f32[192,8192]{1,0:T(8,128)S(1)} %bitcast_dynamic-update-slice_fusion.4, f32[12,8,64,128]{3,2,1,0:T(8,128)S(1)} %bitcast.111), kind=kLoop, calls=%fused_computation.5.clone.1 | loop fusion | bytes 6291456 | tf_op jit(solution)/shard_map/while/body/eval_jaxpr/concatenate | solution.py:54
  55.9 0.0 copy-start
  55.9 2.6 %copy-done = f32[192,8192]{1,0:T(8,128)} copy-done((f32[192,8192]{1,0:T(8,128)}, f32[192,8192]{1,0:T(8,128)S(1)}, u32[]{:S(2)}) %copy-start) | copy-done | bytes 6291480 | tf_op jit(solution)/shard_map/while
  58.5 6.4 %fusion.44 = f32[8192]{0:T(1024)S(1)} fusion(f32[192,8192]{1,0:T(8,128)S(1)} %bitcast_dynamic-update-slice_fusion.5, f32[96,96]{1,0:T(8,128)S(1)} %get-tuple-element.301, f32[96,96]{1,0:T(8,128)S(1)} %get-tuple-element.302, f32[96,96]{1,0:T(8,128)S(1)} %fusion.43), kind=kOutput, calls=%fused_computation.8.clone.1 | convolution fusion | flops 3627126784 | bytes 6434816 | tf_op jit(solution)/shard_map/while/body/eval_jaxpr/dot_general | solution.py:55
  64.9 3.2 %pad_maximum_fusion.3 = f32[192,64,128]{2,1,0:T(8,128)} fusion(f32[96,64,128]{2,1,0:T(8,128)S(1)} %get-tuple-element.300, f32[96,64,128]{2,1,0:T(8,128)S(1)} %get-tuple-element.299), kind=kLoop, calls=%fused_computation.4.clone.1 | loop fusion | flops 1572864 | bytes 12582912 | tf_op jit(solution)/shard_map/while/body/eval_jaxpr/concatenate | solution.py:54
  68.0 7.2 %reshape.257 = f32[2,96,8192]{2,1,0:T(8,128)} reshape(f32[192,64,128]{2,1,0:T(8,128)} %pad_maximum_fusion.3) | data formatting | bytes 12582912 | tf_op jit(solution)/shard_map/while/body/eval_jaxpr/reshape;while/body/eval_jaxpr/reshape | solution.py:57
  75.2 9.0 %fusion.45 = f32[8192]{0:T(1024)S(1)} fusion(f32[2,96,8192]{2,1,0:T(8,128)} %bitcast.110, f32[2,96,8192]{2,1,0:T(8,128)} %reshape.257, f32[3,1,96,96]{3,2,1,0:T(8,128)S(1)} %dynamic-slice_bitcast_fusion.5), kind=kOutput, calls=%fused_computation.7.clone.1 | convolution fusion | flops 1815076864 | bytes 12664832 | tf_op jit(solution)/shard_map/while/body/eval_jaxpr/mn,cnx->cmx/dot_general | solution.py:56
  84.3 0.6 dynamic_slice.62
  84.8 0.6 compare_convert_fusion.2
  85.4 0.2 fusion.42
  85.6 0.1 copy.48
  85.8 0.1 copy.49
  85.8 1.8 %broadcast_multiply_fusion.4 = (f32[96,64,128]{2,1,0:T(8,128)S(1)}, f32[96,64,128]{2,1,0:T(8,128)S(1)}) fusion(f32[96,64]{1,0:T(8,128)S(1)} %copy.48, f32[96,128]{1,0:T(8,128)S(1)} %dynamic-slice_bitcast_fusion.4, f32[96,64]{1,0:T(8,128)S(1)} %copy.49), kind=kLoop, calls=%fused_computation.9.clone.1 | loop fusion | flops 1572864 | bytes 6389760 | tf_op jit(solution)/shard_map/while/body/eval_jaxpr/mul | solution.py:17
  87.7 2.2 %bitcast_dynamic-update-slice_fusion.4 = f32[192,8192]{1,0:T(8,128)S(1)} fusion(f32[12,8,64,128]{3,2,1,0:T(8,128)S(1)} %bitcast.112), kind=kLoop, calls=%fused_computation.6.clone.1 | loop fusion | bytes 6291456 | tf_op jit(solution)/shard_map/while
  89.9 2.2 %bitcast_dynamic-update-slice_fusion.5 = f32[192,8192]{1,0:T(8,128)S(1)} fusion(f32[192,8192]{1,0:T(8,128)S(1)} %bitcast_dynamic-update-slice_fusion.4, f32[12,8,64,128]{3,2,1,0:T(8,128)S(1)} %bitcast.111), kind=kLoop, calls=%fused_computation.5.clone.1 | loop fusion | bytes 6291456 | tf_op jit(solution)/shard_map/while/body/eval_jaxpr/concatenate | solution.py:54
  92.0 0.0 copy-start
  92.1 2.6 %copy-done = f32[192,8192]{1,0:T(8,128)} copy-done((f32[192,8192]{1,0:T(8,128)}, f32[192,8192]{1,0:T(8,128)S(1)}, u32[]{:S(2)}) %copy-start) | copy-done | bytes 6291480 | tf_op jit(solution)/shard_map/while
  94.7 6.4 %fusion.44 = f32[8192]{0:T(1024)S(1)} fusion(f32[192,8192]{1,0:T(8,128)S(1)} %bitcast_dynamic-update-slice_fusion.5, f32[96,96]{1,0:T(8,128)S(1)} %get-tuple-element.301, f32[96,96]{1,0:T(8,128)S(1)} %get-tuple-element.302, f32[96,96]{1,0:T(8,128)S(1)} %fusion.43), kind=kOutput, calls=%fused_computation.8.clone.1 | convolution fusion | flops 3627126784 | bytes 6434816 | tf_op jit(solution)/shard_map/while/body/eval_jaxpr/dot_general | solution.py:55
  101.1 3.2 %pad_maximum_fusion.3 = f32[192,64,128]{2,1,0:T(8,128)} fusion(f32[96,64,128]{2,1,0:T(8,128)S(1)} %get-tuple-element.300, f32[96,64,128]{2,1,0:T(8,128)S(1)} %get-tuple-element.299), kind=kLoop, calls=%fused_computation.4.clone.1 | loop fusion | flops 1572864 | bytes 12582912 | tf_op jit(solution)/shard_map/while/body/eval_jaxpr/concatenate | solution.py:54
  104.2 7.2 %reshape.257 = f32[2,96,8192]{2,1,0:T(8,128)} reshape(f32[192,64,128]{2,1,0:T(8,128)} %pad_maximum_fusion.3) | data formatting | bytes 12582912 | tf_op jit(solution)/shard_map/while/body/eval_jaxpr/reshape;while/body/eval_jaxpr/reshape | solution.py:57
  111.4 9.0 %fusion.45 = f32[8192]{0:T(1024)S(1)} fusion(f32[2,96,8192]{2,1,0:T(8,128)} %bitcast.110, f32[2,96,8192]{2,1,0:T(8,128)} %reshape.257, f32[3,1,96,96]{3,2,1,0:T(8,128)S(1)} %dynamic-slice_bitcast_fusion.5), kind=kOutput, calls=%fused_computation.7.clone.1 | convolution fusion | flops 1815076864 | bytes 12664832 | tf_op jit(solution)/shard_map/while/body/eval_jaxpr/mn,cnx->cmx/dot_general | solution.py:56
  120.4 57.6 %all-reduce = f32[64,128]{1,0:T(8,128)S(1)} all-reduce(f32[64,128]{1,0:T(8,128)S(1)} %broadcast_multiply_fusion.2), channel_id=2, replica_groups=mesh['freq'=16,'grid'=2] {'freq'}, use_global_device_ids=true, to_apply=%region_4.0.clone | all-reduce | flops 8192 | bytes 65536
  178.1 0.6 constant_dynamic-slice_fusion.2
  (17 shorter events, 0.2 us)
Async XLA Ops:
  0.0 48.0 %copy-start.2 = (f32[2,96]{1,0:T(2,128)S(1)}, f32[2,96]{1,0:T(2,128)}, u32[]{:S(2)}) copy-start(f32[2,96]{1,0:T(2,128)} %param.12) | copy-start | bytes 2308
  0.0 48.0 %copy-start.3 = (f32[2,96]{1,0:T(2,128)S(1)}, f32[2,96]{1,0:T(2,128)}, u32[]{:S(2)}) copy-start(f32[2,96]{1,0:T(2,128)} %param.11) | copy-start | bytes 2308
  0.0 48.0 %copy-start.4 = (s32[2]{0:T(128)S(1)}, s32[2]{0:T(128)}, u32[]{:S(2)}) copy-start(s32[2]{0:T(128)} %param.13) | copy-start | bytes 28
  0.0 48.0 %copy-start.1 = (f32[2,96,128]{2,1,0:T(8,128)S(1)}, f32[2,96,128]{2,1,0:T(8,128)}, u32[]{:S(2)}) copy-start(f32[2,96,128]{2,1,0:T(8,128)} %param.10) | copy-start | bytes 294916
  22.6 7.6 %all-to-all-start = ((f32[2,96,128]{2,1,0:T(8,128)}), f32[2,96,128]{2,1,0:T(8,128)S(1)}, u32[]{:S(2)}, u32[]{:S(2)}) async-start(f32[2,96,128]{2,1,0:T(8,128)} %param.9), calls=%async_computation | async-start | bytes 196608 | tf_op jit(solution)/shard_map/all_to_all | solution.py:33
  30.3 10.9 %all-to-all-start.2 = ((f32[2,2,256,128]{3,2,0,1:T(8,128)}), f32[2,2,256,128]{3,2,0,1:T(8,128)S(1)}, u32[]{:S(2)}, u32[]{:S(2)}) async-start(f32[2,2,256,128]{3,2,0,1:T(8,128)} %bitcast.6), calls=%async_computation.2 | async-start | bytes 1048576 | tf_op jit(solution)/shard_map/all_to_all | solution.py:26
  55.9 2.6 %copy-start = (f32[192,8192]{1,0:T(8,128)}, f32[192,8192]{1,0:T(8,128)S(1)}, u32[]{:S(2)}) copy-start(f32[192,8192]{1,0:T(8,128)S(1)} %bitcast_dynamic-update-slice_fusion.5) | copy-start | bytes 18874372 | tf_op jit(solution)/shard_map/while
  92.0 2.6 %copy-start = (f32[192,8192]{1,0:T(8,128)}, f32[192,8192]{1,0:T(8,128)S(1)}, u32[]{:S(2)}) copy-start(f32[192,8192]{1,0:T(8,128)S(1)} %bitcast_dynamic-update-slice_fusion.5) | copy-start | bytes 18874372 | tf_op jit(solution)/shard_map/while
where the time goes:
time: 179 us
  blocking collectives  84.9 us (47%)
  local copies, waits for them, and re-layouts  34 us (19%)
  matrix products  31.9 us (18%)
  other arithmetic  11.6 us (6%)
  waiting for transfers between devices  8.41 us (5%)
  starting transfers between devices  6.83 us (4%)
    unnamed x1, blocking collectives  57.6 us
    all_to_all x1, blocking collectives, per_device(): lax.all_to_all(cross_spectra, 'freq', split_axis=1, concat_axis=2, tiled=...  21.5 us
    dot_general x2, matrix products, one_bin(): jnp.einsum('mn,cnx->cmx', block[2], coefs.reshape(2, modes, count * depth...  18 us
    reshape x2, local copies, waits for them, and re-layouts, one_bin(): coefs.reshape(2, modes, count * depth_here)  14.3 us
    dot_general x2, matrix products, one_bin(): image = jnp.dot(coupling, coefs, precision=HIGH)  12.7 us
    while x6, local copies, waits for them, and re-layouts  9.54 us
    concatenate x2, other arithmetic, one_bin(): jnp.concatenate([coef_real, coef_imag], 0)  6.34 us
    all_gather x1, blocking collectives, per_device(): spectra = lax.all_gather(stacked_local, 'grid', axis=1, tiled=True)  5.81 us
  transfers between devices with their start and end apart: 2, of which 2 were waited for; matrix products, arithmetic and copies ran while one was open for 1% of the time, Pallas kernels for 0%

commit v1 on v0

--- a/solution.py
+++ b/solution.py
@@ -24,7 +24,12 @@
     depth_here = source_modes.shape[2]
     total_bins = bins_here * lax.axis_size("freq")
     whole_spectra = lax.all_to_all(
-        lax.all_to_all(cross_spectra, "freq", split_axis=1, concat_axis=2, tiled=True),
+        jnp.concatenate(
+            lax.all_to_all(
+                jnp.stack(jnp.split(cross_spectra, lax.axis_size("freq"), axis=1)), "freq", 0, 0
+            ),
+            axis=2,
+        ),
         "grid",
         split_axis=1,
         concat_axis=3,

time: 179 us -> 191 us (1.067)
  local copies, waits for them, and re-layouts: 34 us -> 45.1 us
    unnamed x11 -> x25, local copies, waits for them, and re-layouts: 3.04 us -> 13.4 us
where the time goes in v1:
time: 191 us; the launch traced here: 190 us
  blocking collectives  84.9 us (44%)
  local copies, waits for them, and re-layouts  45.1 us (24%)
  matrix products  31.9 us (17%)
  other arithmetic  11.6 us (6%)
  waiting for transfers between devices  8.38 us (4%)
  starting transfers between devices  6.83 us (4%)
    unnamed x1, blocking collectives  57.6 us
    all_to_all x1, blocking collectives, per_device(): lax.all_to_all(jnp.stack(jnp.split(cross_spectra, lax.axis_size('freq'),...  21.5 us
    dot_general x2, matrix products, one_bin(): jnp.einsum('mn,cnx->cmx', block[2], coefs.reshape(2, modes, count * depth...  18 us
    reshape x2, local copies, waits for them, and re-layouts, one_bin(): coefs.reshape(2, modes, count * depth_here)  14.3 us
    unnamed x25, local copies, waits for them, and re-layouts  13.4 us
    dot_general x2, matrix products, one_bin(): image = jnp.dot(coupling, coefs, precision=HIGH)  12.7 us
    while x6, local copies, waits for them, and re-layouts  9.54 us
    concatenate x2, other arithmetic, one_bin(): jnp.concatenate([coef_real, coef_imag], 0)  6.34 us
  transfers between devices with their start and end apart: 2, of which 2 were waited for; matrix products, arithmetic and copies ran while one was open for 1% of the time, Pallas kernels for 0%

profile of v1, /device:TPU:0, one launch (start us, length us, event | category | flops | bytes accessed | tf_op | source)
XLA Modules:
  0.0 189.8 jit_solution(9682889852274238373)
XLA Ops:
  0.0 0.8 constant_dynamic-update-slice_fusion.15
  0.8 0.8 constant_dynamic-update-slice_fusion.14
  1.6 0.8 constant_dynamic-update-slice_fusion.13
  2.3 0.8 constant_dynamic-update-slice_fusion.12
  3.1 0.8 constant_dynamic-update-slice_fusion.11
  3.9 0.8 constant_dynamic-update-slice_fusion.10
  4.6 0.8 constant_dynamic-update-slice_fusion.9
  5.4 0.8 constant_dynamic-update-slice_fusion.8
  6.1 0.8 constant_dynamic-update-slice_fusion.7
  6.9 0.8 constant_dynamic-update-slice_fusion.6
  7.7 0.8 constant_dynamic-update-slice_fusion.5
  8.4 0.8 constant_dynamic-update-slice_fusion.4
  9.2 0.8 constant_dynamic-update-slice_fusion.3
  10.0 0.8 constant_dynamic-update-slice_fusion.2
  10.7 0.8 constant_dynamic-update-slice_fusion.1
  11.5 0.8 constant_dynamic-update-slice_fusion
  12.2 21.5 %all_to_all.35 = f32[16,2,2,16,128]{4,3,2,1,0:T(8,128)S(1)} all-to-all(f32[16,2,2,16,128]{4,3,2,1,0:T(8,128)S(1)} %constant_dynamic-update-slice_fusion), channel_id=1, replica_groups=mesh['freq'=16,'grid'=2] {'freq'}, dimensions={0} | all-to-all | bytes 1048576 | tf_op jit(solution)/shard_map/all_to_all | solution.py:28
  33.7 3.3 %all-to-all-start.2 = ((f32[2,96,128]{2,1,0:T(8,128)}), f32[2,96,128]{2,1,0:T(8,128)S(1)}, u32[]{:S(2)}, u32[]{:S(2)}) async-start(f32[2,96,128]{2,1,0:T(8,128)} %param.9), calls=%async_computation.2 | async-start | bytes 196608 | tf_op jit(solution)/shard_map/all_to_all | solution.py:38
  37.1 0.8 copy.29
  37.9 3.4 %all-to-all-done.2 = f32[2,96,128]{2,1,0:T(8,128)S(1)} async-done(((f32[2,96,128]{2,1,0:T(8,128)}), f32[2,96,128]{2,1,0:T(8,128)S(1)}, u32[]{:S(2)}, u32[]{:S(2)}) %all-to-all-start.2) | async-done | bytes 98336 | tf_op jit(solution)/shard_map/all_to_all | solution.py:38
  41.3 3.5 %all-to-all-start.1 = ((f32[2,2,256,128]{3,2,0,1:T(8,128)}), f32[2,2,256,128]{3,2,0,1:T(8,128)S(1)}, u32[]{:S(2)}, u32[]{:S(2)}) async-start(f32[2,2,256,128]{3,2,0,1:T(8,128)} %copy.29), calls=%async_computation.1 | async-start | bytes 1048576 | tf_op jit(solution)/shard_map/all_to_all | solution.py:26
  44.8 1.3 dynamic-slice
  46.8 0.1 copy.31
  46.9 0.1 reshape.257
  47.0 0.2 convolution_bitcast_fusion.3
  47.3 5.0 %all-to-all-done.1 = f32[2,2,256,128]{3,2,0,1:T(8,128)S(1)} async-done(((f32[2,2,256,128]{3,2,0,1:T(8,128)}), f32[2,2,256,128]{3,2,0,1:T(8,128)S(1)}, u32[]{:S(2)}, u32[]{:S(2)}) %all-to-all-start.1) | async-done | bytes 524320 | tf_op jit(solution)/shard_map/all_to_all | solution.py:26
  52.2 0.6 convolution_bitcast_fusion.1
  52.9 0.3 convolution_bitcast_fusion.2
  53.2 0.1 copy.33
  53.3 5.8 %all_gather.3 = f32[3,2,96,96]{3,2,0,1:T(8,128)S(1)} all-gather(f32[3,1,96,96]{3,2,0,1:T(8,128)S(1)} %copy.33), channel_id=1, replica_groups=mesh['freq'=16,'grid'=2] {'grid'}, dimensions={1}, use_global_device_ids=true | all-gather | bytes 331776 | tf_op jit(solution)/shard_map/all_gather | solution.py:43
  59.2 0.0 copy-done.2
  59.2 0.0 copy-done.3
  59.2 0.0 copy-done.4
  59.2 0.0 copy-done.1
  59.2 72.4 %while.15 = (s32[]{:T(128)}, f32[64,128]{1,0:T(8,128)S(1)}, f32[2,96]{1,0:T(2,128)S(1)}, f32[2,96]{1,0:T(2,128)S(1)}, s32[2]{0:T(128)S(1)}, /*index=5*/f32[2,96,...) while((s32[]{:T(128)}, f32[64,128]{1,0:T(8,128)S(1)}, ...), condition=%wide.region_3.0_spmd.clone.clone, body=%wide.region_0.0_spmd.clone.clone.sunk | while | flops 5445426688 | bytes 89226920 | solution.py:69
  59.2 0.6 dynamic_slice.62
  59.8 0.6 compare_convert_fusion.2
  60.4 0.2 fusion.42
  60.6 0.1 copy.53
  60.7 0.1 copy.54
  60.8 1.8 broadcast_multiply_fusion.4
  62.6 2.2 %bitcast_dynamic-update-slice_fusion.4 = f32[192,8192]{1,0:T(8,128)S(1)} fusion(f32[12,8,64,128]{3,2,1,0:T(8,128)S(1)} %bitcast.138), kind=kLoop, calls=%fused_computation.6.clone.1 | loop fusion | bytes 6291456 | tf_op jit(solution)/shard_map/while
  64.8 2.2 %bitcast_dynamic-update-slice_fusion.5 = f32[192,8192]{1,0:T(8,128)S(1)} fusion(f32[192,8192]{1,0:T(8,128)S(1)} %bitcast_dynamic-update-slice_fusion.4, f32[12,8,64,128]{3,2,1,0:T(8,128)S(1)} %bitcast.137), kind=kLoop, calls=%fused_computation.5.clone.1 | loop fusion | bytes 6291456 | tf_op jit(solution)/shard_map/while/body/eval_jaxpr/concatenate | solution.py:59
  67.0 0.0 copy-start
  67.0 2.6 %copy-done = f32[192,8192]{1,0:T(8,128)} copy-done((f32[192,8192]{1,0:T(8,128)}, f32[192,8192]{1,0:T(8,128)S(1)}, u32[]{:S(2)}) %copy-start) | copy-done | bytes 6291480 | tf_op jit(solution)/shard_map/while
  69.6 6.4 %fusion.44 = f32[8192]{0:T(1024)S(1)} fusion(f32[192,8192]{1,0:T(8,128)S(1)} %bitcast_dynamic-update-slice_fusion.5, f32[96,96]{1,0:T(8,128)S(1)} %get-tuple-element.308, f32[96,96]{1,0:T(8,128)S(1)} %get-tuple-element.309, f32[96,96]{1,0:T(8,128)S(1)} %fusion.43), kind=kOutput, calls=%fused_computation.8.clone.1 | convolution fusion | flops 3627126784 | bytes 6434816 | tf_op jit(solution)/shard_map/while/body/eval_jaxpr/dot_general | solution.py:60
  76.0 3.2 %pad_maximum_fusion.3 = f32[192,64,128]{2,1,0:T(8,128)} fusion(f32[96,64,128]{2,1,0:T(8,128)S(1)} %get-tuple-element.307, f32[96,64,128]{2,1,0:T(8,128)S(1)} %get-tuple-element.306), kind=kLoop, calls=%fused_computation.4.clone.1 | loop fusion | flops 1572864 | bytes 12582912 | tf_op jit(solution)/shard_map/while/body/eval_jaxpr/concatenate | solution.py:59
  79.2 7.2 %reshape.262 = f32[2,96,8192]{2,1,0:T(8,128)} reshape(f32[192,64,128]{2,1,0:T(8,128)} %pad_maximum_fusion.3) | data formatting | bytes 12582912 | tf_op jit(solution)/shard_map/while/body/eval_jaxpr/reshape;while/body/eval_jaxpr/reshape | solution.py:62
  86.3 9.0 %fusion.45 = f32[8192]{0:T(1024)S(1)} fusion(f32[2,96,8192]{2,1,0:T(8,128)} %bitcast.136, f32[2,96,8192]{2,1,0:T(8,128)} %reshape.262, f32[3,1,96,96]{3,2,1,0:T(8,128)S(1)} %dynamic-slice_bitcast_fusion.5), kind=kOutput, calls=%fused_computation.7.clone.1 | convolution fusion | flops 1815076864 | bytes 12664832 | tf_op jit(solution)/shard_map/while/body/eval_jaxpr/mn,cnx->cmx/dot_general | solution.py:61
  95.4 0.6 dynamic_slice.62
  96.0 0.6 compare_convert_fusion.2
  96.5 0.2 fusion.42
  96.8 0.1 copy.53
  96.9 0.1 copy.54
  97.0 1.8 broadcast_multiply_fusion.4
  98.8 2.2 %bitcast_dynamic-update-slice_fusion.4 = f32[192,8192]{1,0:T(8,128)S(1)} fusion(f32[12,8,64,128]{3,2,1,0:T(8,128)S(1)} %bitcast.138), kind=kLoop, calls=%fused_computation.6.clone.1 | loop fusion | bytes 6291456 | tf_op jit(solution)/shard_map/while
  101.0 2.2 %bitcast_dynamic-update-slice_fusion.5 = f32[192,8192]{1,0:T(8,128)S(1)} fusion(f32[192,8192]{1,0:T(8,128)S(1)} %bitcast_dynamic-update-slice_fusion.4, f32[12,8,64,128]{3,2,1,0:T(8,128)S(1)} %bitcast.137), kind=kLoop, calls=%fused_computation.5.clone.1 | loop fusion | bytes 6291456 | tf_op jit(solution)/shard_map/while/body/eval_jaxpr/concatenate | solution.py:59
  103.2 2.6 %copy-done = f32[192,8192]{1,0:T(8,128)} copy-done((f32[192,8192]{1,0:T(8,128)}, f32[192,8192]{1,0:T(8,128)S(1)}, u32[]{:S(2)}) %copy-start) | copy-done | bytes 6291480 | tf_op jit(solution)/shard_map/while
  105.8 6.4 %fusion.44 = f32[8192]{0:T(1024)S(1)} fusion(f32[192,8192]{1,0:T(8,128)S(1)} %bitcast_dynamic-update-slice_fusion.5, f32[96,96]{1,0:T(8,128)S(1)} %get-tuple-element.308, f32[96,96]{1,0:T(8,128)S(1)} %get-tuple-element.309, f32[96,96]{1,0:T(8,128)S(1)} %fusion.43), kind=kOutput, calls=%fused_computation.8.clone.1 | convolution fusion | flops 3627126784 | bytes 6434816 | tf_op jit(solution)/shard_map/while/body/eval_jaxpr/dot_general | solution.py:60
  112.2 3.2 %pad_maximum_fusion.3 = f32[192,64,128]{2,1,0:T(8,128)} fusion(f32[96,64,128]{2,1,0:T(8,128)S(1)} %get-tuple-element.307, f32[96,64,128]{2,1,0:T(8,128)S(1)} %get-tuple-element.306), kind=kLoop, calls=%fused_computation.4.clone.1 | loop fusion | flops 1572864 | bytes 12582912 | tf_op jit(solution)/shard_map/while/body/eval_jaxpr/concatenate | solution.py:59
  115.3 7.2 %reshape.262 = f32[2,96,8192]{2,1,0:T(8,128)} reshape(f32[192,64,128]{2,1,0:T(8,128)} %pad_maximum_fusion.3) | data formatting | bytes 12582912 | tf_op jit(solution)/shard_map/while/body/eval_jaxpr/reshape;while/body/eval_jaxpr/reshape | solution.py:62
  122.5 9.0 %fusion.45 = f32[8192]{0:T(1024)S(1)} fusion(f32[2,96,8192]{2,1,0:T(8,128)} %bitcast.136, f32[2,96,8192]{2,1,0:T(8,128)} %reshape.262, f32[3,1,96,96]{3,2,1,0:T(8,128)S(1)} %dynamic-slice_bitcast_fusion.5), kind=kOutput, calls=%fused_computation.7.clone.1 | convolution fusion | flops 1815076864 | bytes 12664832 | tf_op jit(solution)/shard_map/while/body/eval_jaxpr/mn,cnx->cmx/dot_general | solution.py:61
  131.6 57.6 %all-reduce = f32[64,128]{1,0:T(8,128)S(1)} all-reduce(f32[64,128]{1,0:T(8,128)S(1)} %broadcast_multiply_fusion.2), channel_id=2, replica_groups=mesh['freq'=16,'grid'=2] {'freq'}, use_global_device_ids=true, to_apply=%region_4.0.clone | all-reduce | flops 8192 | bytes 65536
  189.2 0.6 constant_dynamic-slice_fusion.2
  (23 shorter events, 0.2 us)
Async XLA Ops:
  0.0 59.2 %copy-start.2 = (f32[2,96]{1,0:T(2,128)S(1)}, f32[2,96]{1,0:T(2,128)}, u32[]{:S(2)}) copy-start(f32[2,96]{1,0:T(2,128)} %param.12) | copy-start | bytes 2308
  0.0 59.2 %copy-start.3 = (f32[2,96]{1,0:T(2,128)S(1)}, f32[2,96]{1,0:T(2,128)}, u32[]{:S(2)}) copy-start(f32[2,96]{1,0:T(2,128)} %param.11) | copy-start | bytes 2308
  0.0 59.2 %copy-start.4 = (s32[2]{0:T(128)S(1)}, s32[2]{0:T(128)}, u32[]{:S(2)}) copy-start(s32[2]{0:T(128)} %param.13) | copy-start | bytes 28
  0.0 59.2 %copy-start.1 = (f32[2,96,128]{2,1,0:T(8,128)S(1)}, f32[2,96,128]{2,1,0:T(8,128)}, u32[]{:S(2)}) copy-start(f32[2,96,128]{2,1,0:T(8,128)} %param.10) | copy-start | bytes 294916
  33.7 7.6 %all-to-all-start.2 = ((f32[2,96,128]{2,1,0:T(8,128)}), f32[2,96,128]{2,1,0:T(8,128)S(1)}, u32[]{:S(2)}, u32[]{:S(2)}) async-start(f32[2,96,128]{2,1,0:T(8,128)} %param.9), calls=%async_computation.2 | async-start | bytes 196608 | tf_op jit(solution)/shard_map/all_to_all | solution.py:38
  41.3 10.9 %all-to-all-start.1 = ((f32[2,2,256,128]{3,2,0,1:T(8,128)}), f32[2,2,256,128]{3,2,0,1:T(8,128)S(1)}, u32[]{:S(2)}, u32[]{:S(2)}) async-start(f32[2,2,256,128]{3,2,0,1:T(8,128)} %copy.29), calls=%async_computation.1 | async-start | bytes 1048576 | tf_op jit(solution)/shard_map/all_to_all | solution.py:26
  67.0 2.6 %copy-start = (f32[192,8192]{1,0:T(8,128)}, f32[192,8192]{1,0:T(8,128)S(1)}, u32[]{:S(2)}) copy-start(f32[192,8192]{1,0:T(8,128)S(1)} %bitcast_dynamic-update-slice_fusion.5) | copy-start | bytes 18874372 | tf_op jit(solution)/shard_map/while
  103.2 2.6 %copy-start = (f32[192,8192]{1,0:T(8,128)}, f32[192,8192]{1,0:T(8,128)S(1)}, u32[]{:S(2)}) copy-start(f32[192,8192]{1,0:T(8,128)S(1)} %bitcast_dynamic-update-slice_fusion.5) | copy-start | bytes 18874372 | tf_op jit(solution)/shard_map/while
